TPU v7x, 128 devices: a whole 4x4x4 slice. The times are simulated.
128 devices in a mesh: dp: 8 (over x, core), tensor: 16 (over y, z).
Axes of the slice: x: 4, y: 4, z: 4, core: 2. Of those that a mesh axis runs over, the one named last changes fastest.
Arguments:
- hidden: bfloat16 [16, 64, 4608], P('dp', 'tensor'), may hold values from -6 to 6
- gain: float32 [4608], replicated, may hold values from 0.5 to 1.5
- labels: int32 [16, 64], P('dp', 'tensor'), may hold values from 0 to 255999
- lengths: int32 [16], replicated, may hold values from 1 to 64
- embed: bfloat16 [256000, 4608], P(('dp', 'tensor')), may hold values from -0.375 to 0.375
Outputs:
- token_logprob: float32 [16, 64], P('dp', 'tensor')
- mean_nll: float32 [], replicated
- z_loss: float32 [], replicated
All inputs are finite; a program needn't handle non-finite values.
Results may differ from a plain program's by a relative error of at most 0.00058.
Values may be sent and summed in bfloat16 or wider, within the bound.
No kernel may reach another device: no remote copies, remote signals or barrier semaphores. Data moves between devices by JAX's collectives and lax.ppermute only.
A program may use at most 128 MiB of HBM per device.

v0:
```python
import jax
import jax.numpy as jnp
from jax import lax
from jax.sharding import Mesh
from jax.sharding import PartitionSpec as P

CAP = 30
TENSOR = ("tensor_0", "tensor_1")
DP = ("dp_0", "dp_1")
DP_TENSOR = ("dp_0", "dp_1", "tensor_0", "tensor_1")


def joined_along(pieces, dim):
    lengths = list(pieces.shape[1:])
    lengths[dim] *= pieces.shape[0]
    return jnp.moveaxis(pieces, 0, dim).reshape(lengths)


def gather_in_order(value, axes, order):
    pieces = value[None]
    for k in order:
        pieces = lax.all_gather(pieces, axes[k], axis=0, tiled=True)
    block = [lax.axis_size(axes[k]) for k in reversed(order)]
    pieces = pieces.reshape(*block, *value.shape)
    turned = sorted(range(len(order)), key=lambda place: order[len(order) - 1 - place])
    return pieces.transpose(*turned, *range(len(order), pieces.ndim)).reshape(-1, *value.shape)


def gathered_by_axis(value, axes, order, dim):
    return joined_along(gather_in_order(value, axes, order), dim)


def one_axis_at_a_time(value, axes):
    for axis in axes:
        value = lax.psum(value, axis)
    return value


def normalize(rows, gain):
    values = rows.astype(jnp.float32)
    meansq = jnp.mean(values * values, axis=-1, keepdims=True)
    return (values * lax.rsqrt(meansq + 1e-06) * gain).astype(jnp.bfloat16)


def per_device(hidden, gain, labels, lengths, embed):
    n_tensor = lax.axis_size(TENSOR)
    n_all = lax.axis_size(DP) * n_tensor
    seqs, stretch, width = hidden.shape
    vocab_dev = embed.shape[0]
    rows_local = seqs * stretch
    total_rows = rows_local * n_all
    flat = hidden.reshape(rows_local, width)
    row_ids = jnp.arange(total_rows)
    owner = row_ids // rows_local
    within = row_ids % rows_local
    batch_ids = owner // n_tensor * seqs + within // stretch
    positions = owner % n_tensor * stretch + within % stretch
    live_all = (positions < jnp.take(lengths, batch_ids)).astype(jnp.float32)
    all_labels = gathered_by_axis(labels.reshape(rows_local), DP_TENSOR, (0, 2, 3, 1), 0)
    rows = normalize(lax.all_gather(flat, DP_TENSOR, axis=0, tiled=True), gain)
    values = lax.dot_general(
        rows, embed, (((1,), (1,)), ((), ())), preferred_element_type=jnp.float32
    )
    capped = CAP * jnp.tanh(values / CAP)
    sumexp = jnp.sum(jnp.exp(capped), axis=1)
    first = lax.axis_index(DP_TENSOR) * vocab_dev
    local = all_labels - first
    inside = (local >= 0) & (local < vocab_dev)
    chosen = jnp.take_along_axis(capped, jnp.clip(local, 0, vocab_dev - 1)[:, None], axis=1)[:, 0]
    picked = jnp.where(inside, chosen, jnp.float32(0.0))
    own_start = lax.axis_index(DP_TENSOR) * rows_local
    sum_total, pick_total = (
        one_axis_at_a_time(sumexp, DP_TENSOR),
        one_axis_at_a_time(picked, DP_TENSOR),
    )
    own_sum = lax.dynamic_slice_in_dim(sum_total, own_start, rows_local)
    own_pick = lax.dynamic_slice_in_dim(pick_total, own_start, rows_local)
    own_live = lax.dynamic_slice_in_dim(live_all, own_start, rows_local)
    lse = jnp.log(own_sum)
    token = own_live * (own_pick - lse)
    nll_sum, count, square_sum = (
        one_axis_at_a_time(-jnp.sum(token), DP_TENSOR),
        one_axis_at_a_time(jnp.sum(own_live), DP_TENSOR),
        one_axis_at_a_time(jnp.sum(own_live * lse * lse), DP_TENSOR),
    )
    mean_nll = nll_sum / count
    z_loss = 0.01 * square_sum / count
    return (token.reshape(seqs, stretch), mean_nll, z_loss)


def solution(mesh):
    finer = Mesh(mesh.devices.reshape(4, 2, 4, 4), ("dp_0", "dp_1", "tensor_0", "tensor_1"))
    placed = (P(DP, TENSOR, None), P(), P(DP, TENSOR), P(), P(DP_TENSOR, None))
    return jax.shard_map(
        per_device,
        mesh=finer,
        in_specs=placed,
        out_specs=(P(DP, TENSOR), P(), P()),
        check_vma=False,
    )
```

profile of v0, /device:TPU:0, one launch (start us, length us, event | category | flops | bytes accessed | tf_op | source)
XLA Modules:
  0.0 235.7 jit_solution(905636388065802860)
XLA Ops:
  7.2 0.0 copy-start.1
  7.2 0.0 all-gather.6.cloned.1.call-start
  7.2 1.5 reshape.258
  8.8 0.0 all-gather.6.cloned.1.call-update
  8.8 0.8 reshape.330
  9.5 9.8 %all-gather = s32[4,1,8]{2,1,0:T(1,128)S(1)} all-gather(s32[1,1,8]{2,1,0:T(1,128)S(1)} %reshape.330), channel_id=1, replica_groups=mesh['dp_0'=4,'dp_1'=2,'tensor_0'=4,'tensor_1'=4] {'dp_0'}, dimensions={0}, use_global_device_ids=true | all-gather | bytes 160 | tf_op jit(solution)/shard_map/all_gather | solution.py:22
  19.4 11.3 %all-gather.1 = s32[4,4,8]{2,1,0:T(4,128)S(1)} all-gather(s32[1,4,8]{2,1,0:T(4,128)S(1)} %bitcast.36), channel_id=1, replica_groups=mesh['dp_0'=4,'dp_1'=2,'tensor_0'=4,'tensor_1'=4] {'tensor_0'}, dimensions={0}, use_global_device_ids=true | all-gather | bytes 640 | tf_op jit(solution)/shard_map/all_gather | solution.py:22
  30.7 0.1 copy.22
  30.8 13.2 %all-gather.2 = s32[4,16,8]{1,2,0:T(8,128)S(1)} all-gather(s32[1,16,8]{1,2,0:T(8,128)S(1)} %copy.22), channel_id=1, replica_groups=mesh['dp_0'=4,'dp_1'=2,'tensor_0'=4,'tensor_1'=4] {'tensor_1'}, dimensions={0}, use_global_device_ids=true | all-gather | bytes 2560 | tf_op jit(solution)/shard_map/all_gather | solution.py:22
  44.0 0.1 reshape.336
  44.1 1.8 all-gather.3
  45.9 0.1 copy.26
  46.0 0.1 min.24
  46.1 0.1 min.22
  46.2 0.1 copy.24
  46.4 0.1 and.146
  46.5 0.1 compare_reduce_fusion
  46.6 0.1 compare_reduce_fusion.1
  46.6 0.1 compare_reduce_fusion.2
  46.7 0.1 compare_reduce_fusion.3
  46.7 0.1 compare_reduce_fusion.4
  46.8 0.1 compare_reduce_fusion.5
  46.8 0.1 compare_reduce_fusion.6
  46.9 0.1 compare_reduce_fusion.7
  47.0 0.1 compare_reduce_fusion.8
  47.0 2.0 fusion.37
  49.0 4.4 %compare_select_fusion.2 = s32[1024,1]{0,1:T(1,128)S(1)} fusion(s32[]{:T(128)} %bitcast.9, s32[]{:T(128)} %bitcast.10, s32[]{:T(128)} %bitcast.11, s32[]{:T(128)} %bitcast.12, s32[]{:T(128)} %bitcast.13, s32[]{:T(128)} %bitcast.15, s32[]{:T(128)} %bitcast.14), kind=kLoop, calls=%fused_computation.22 | loop fusion | flops 60416 | bytes 4124 | tf_op jit(solution)/shard_map/jit(_take)/gather | solution.py:58
  53.5 5.8 %fusion.34 = f32[1024]{0:T(1024)S(1)} fusion(pred[1024]{0:T(1024)(128)(4,1)S(1)} %compare_reduce_fusion, pred[1024]{0:T(1024)(128)(4,1)S(1)} %compare_reduce_fusion.1, pred[1024]{0:T(1024)(128)(4,1)S(1)} %compare_reduce_fusion.2, pred[1024]{0:T(1024)(128)(4,1)S(1)} %compare_reduce_fusion.3, pred[1024]{0:T(1024)(128)(4,1)S(1)} %compare_reduce_fusion.4, ...), kind=kLoop, calls=%fused_computation.90 | loop fusion | flops 73728 | bytes 17444 | tf_op jit(solution)/shard_map/convert_element_type | solution.py:58
  59.3 24.7 %all-gather.6.cloned.1.call-done = bf16[1024,4608]{1,0:T(8,128)(2,1)} async-done(((bf16[8,4608]{1,0:T(8,128)(2,1)}), bf16[1024,4608]{1,0:T(8,128)(2,1)}) %all-gather.6.cloned.1.call-update) | async-done | bytes 9437200 | tf_op jit(solution)/shard_map/all_gather | solution.py:60
  84.0 0.0 copy-start
  84.0 5.7 %fusion = f32[1024]{0:T(1024)S(1)} fusion(bf16[1024,4608]{1,0:T(8,128)(2,1)} %all-gather.6.cloned.1.call-done), kind=kLoop, calls=%fused_computation.3 | loop fusion | flops 14154752 | bytes 9441280 | tf_op jit(solution)/shard_map/reduce_sum | solution.py:41
  89.7 0.0 copy-done.1
  89.7 0.6 copy-done
  90.3 26.1 %exponential_reduce_fusion = (f32[1024]{0:T(1024)S(1)}, f32[1024,2000]{0,1:T(8,128)}) fusion(bf16[2000,4608]{1,0:T(8,128)(2,1)} %param.9, bf16[1024,4608]{1,0:T(8,128)(2,1)S(1)} %copy-done, f32[4608]{0:T(1024)S(1)} %copy-done.1, f32[1024]{0:T(1024)S(1)} %add_rsqrt_fusion), kind=kOutput, calls=%fused_computation.9 | convolution fusion | flops 18899386368 | bytes 36087808 | tf_op jit(solution)/shard_map/dot_general | solution.py:61
  116.4 45.1 %gather_fusion = f32[1024]{0:T(1024)S(1)} fusion(f32[1024,2000]{0,1:T(8,128)} %get-tuple-element.46, s32[1024]{0:T(1024)S(1)} %bitcast.31), kind=kCustom, calls=%fused_computation | custom fusion | bytes 16384 | tf_op jit(solution)/shard_map/jit(take_along_axis)/gather | solution.py:69
  161.5 7.8 %all-reduce.5 = (f32[1024]{0:T(1024)S(1)}, f32[1024]{0:T(1024)S(1)}) all-reduce(f32[1024]{0:T(1024)S(1)} %select_select_fusion.1, f32[1024]{0:T(1024)S(1)} %get-tuple-element.45), channel_id=1, replica_groups=mesh['dp_0'=4,'dp_1'=2,'tensor_0'=4,'tensor_1'=4] {'dp_0'}, use_global_device_ids=true, to_apply=%region_1.2 | all-reduce | flops 2048 | bytes 16384 | tf_op jit(solution)/shard_map/psum | solution.py:35
  169.4 2.5 %all-reduce.7 = (f32[1024]{0:T(1024)S(1)}, f32[1024]{0:T(1024)S(1)}) all-reduce(f32[1024]{0:T(1024)S(1)} %get-tuple-element.18, f32[1024]{0:T(1024)S(1)} %get-tuple-element.19), channel_id=1, replica_groups=mesh['dp_0'=4,'dp_1'=2,'tensor_0'=4,'tensor_1'=4] {'dp_1'}, use_global_device_ids=true, to_apply=%region_2.3 | all-reduce | flops 2048 | bytes 16384 | tf_op jit(solution)/shard_map/psum | solution.py:35
  171.9 8.4 %all-reduce.3 = (f32[1024]{0:T(1024)S(1)}, f32[1024]{0:T(1024)S(1)}) all-reduce(f32[1024]{0:T(1024)S(1)} %get-tuple-element.23, f32[1024]{0:T(1024)S(1)} %get-tuple-element.24), channel_id=1, replica_groups=mesh['dp_0'=4,'dp_1'=2,'tensor_0'=4,'tensor_1'=4] {'tensor_0'}, use_global_device_ids=true, to_apply=%region_3.4 | all-reduce | flops 2048 | bytes 16384 | tf_op jit(solution)/shard_map/psum | solution.py:35
  180.3 10.1 %all-reduce.1 = (f32[1024]{0:T(1024)S(1)}, f32[1024]{0:T(1024)S(1)}) all-reduce(f32[1024]{0:T(1024)S(1)} %get-tuple-element.13, f32[1024]{0:T(1024)S(1)} %get-tuple-element.14), channel_id=1, replica_groups=mesh['dp_0'=4,'dp_1'=2,'tensor_0'=4,'tensor_1'=4] {'tensor_1'}, use_global_device_ids=true, to_apply=%region_4.5 | all-reduce | flops 2048 | bytes 16384 | tf_op jit(solution)/shard_map/psum | solution.py:35
  190.4 0.8 fusion.35
  191.2 0.6 reshape.259
  192.5 8.5 %all-reduce.4 = (f32[]{:T(128)}, f32[]{:T(128)}, f32[]{:T(128)}) all-reduce(f32[]{:T(128)S(6)} %neg.3, f32[]{:T(128)} %get-tuple-element.4, f32[]{:T(128)} %get-tuple-element.3), channel_id=1, replica_groups=mesh['dp_0'=4,'dp_1'=2,'tensor_0'=4,'tensor_1'=4] {'dp_0'}, use_global_device_ids=true, to_apply=%region_11.12 | all-reduce | flops 3 | bytes 24 | tf_op jit(solution)/shard_map/psum | solution.py:35
  201.0 3.1 %all-reduce.6 = (f32[]{:T(128)}, f32[]{:T(128)}, f32[]{:T(128)}) all-reduce(f32[]{:T(128)} %get-tuple-element.15, f32[]{:T(128)} %get-tuple-element.16, f32[]{:T(128)} %get-tuple-element.17), channel_id=1, replica_groups=mesh['dp_0'=4,'dp_1'=2,'tensor_0'=4,'tensor_1'=4] {'dp_1'}, use_global_device_ids=true, to_apply=%region_12.13 | all-reduce | flops 3 | bytes 24 | tf_op jit(solution)/shard_map/psum | solution.py:35
  204.1 10.3 %all-reduce.2 = (f32[]{:T(128)}, f32[]{:T(128)}, f32[]{:T(128)}) all-reduce(f32[]{:T(128)} %get-tuple-element.20, f32[]{:T(128)} %get-tuple-element.21, f32[]{:T(128)} %get-tuple-element.22), channel_id=1, replica_groups=mesh['dp_0'=4,'dp_1'=2,'tensor_0'=4,'tensor_1'=4] {'tensor_0'}, use_global_device_ids=true, to_apply=%region_13.14 | all-reduce | flops 3 | bytes 24 | tf_op jit(solution)/shard_map/psum | solution.py:35
  214.4 9.7 %all-reduce = (f32[]{:T(128)}, f32[]{:T(128)}, f32[]{:T(128)}) all-reduce(f32[]{:T(128)} %get-tuple-element.10, f32[]{:T(128)} %get-tuple-element.11, f32[]{:T(128)} %get-tuple-element.12), channel_id=1, replica_groups=mesh['dp_0'=4,'dp_1'=2,'tensor_0'=4,'tensor_1'=4] {'tensor_1'}, use_global_device_ids=true, to_apply=%region_14.15 | all-reduce | flops 3 | bytes 24 | tf_op jit(solution)/shard_map/psum | solution.py:35
  (11 shorter events, 0.1 us)
Async XLA Ops:
  7.2 82.6 %copy-start.1 = (f32[4608]{0:T(1024)S(1)}, f32[4608]{0:T(1024)}, u32[]{:S(2)}) copy-start(f32[4608]{0:T(1024)} %param.6) | copy-start | bytes 55300
  7.2 76.8 %all-gather.6.cloned.1.call-start = ((), (), s32[]{:S(2)}) async-start(), calls=%async_computation | async-start | bytes 9510912 | tf_op jit(solution)/shard_map/all_gather | solution.py:60
  84.0 6.4 %copy-start = (bf16[1024,4608]{1,0:T(8,128)(2,1)S(1)}, bf16[1024,4608]{1,0:T(8,128)(2,1)}, u32[]{:S(2)}) copy-start(bf16[1024,4608]{1,0:T(8,128)(2,1)} %all-gather.6.cloned.1.call-done) | copy-start | bytes 28311556
Sparse Core Ops, SparseCore 0:
  11.1 72.8 all-gather.5
where the time goes:
time: 237 us; the launch traced here: 236 us
  blocking collectives  96.5 us (41%)
  local copies, waits for them, and re-layouts  51.3 us (22%)
  matrix products  26.1 us (11%)
  waiting for transfers between devices  24.7 us (10%)
  between operations  19.7 us (8%)
  other arithmetic  17.3 us (7%)
    psum x8, blocking collectives, one_axis_at_a_time(): value = lax.psum(value, axis)  60.4 us
    gather x1, local copies, waits for them, and re-layouts, per_device(): jnp.take_along_axis(capped, jnp.clip(local, 0, vocab_dev - 1)[:, None], a...  45.1 us
    all_gather x4, blocking collectives, gather_in_order(): pieces = lax.all_gather(pieces, axes[k], axis=0, tiled=True)  36.2 us
    dot_general x1, matrix products, per_device(): lax.dot_general(rows, embed, (((1,), (1,)), ((), ())), preferred_element_...  26.1 us
    all_gather x1, waiting for transfers between devices, per_device(): rows = normalize(lax.all_gather(flat, DP_TENSOR, axis=0, tiled=True), gain)  24.7 us
    convert_element_type x1, other arithmetic, per_device(): live_all = (positions < jnp.take(lengths, batch_ids)).astype(jnp.float32)  5.82 us
    reduce_sum x1, other arithmetic, normalize(): meansq = jnp.mean(values * values, axis=-1, keepdims=True)  5.72 us
    gather x10, other arithmetic, per_device(): live_all = (positions < jnp.take(lengths, batch_ids)).astype(jnp.float32)  4.91 us
  transfers between devices with their start and end apart: 1, of which 1 were waited for; matrix products, arithmetic and copies ran while one was open for 6% of the time, Pallas kernels for 0%

commit v1 on v0

--- a/solution.py
+++ b/solution.py
@@ -32,7 +32,7 @@
 
 def one_axis_at_a_time(value, axes):
     for axis in axes:
-        value = lax.psum(value, axis)
+        value = jnp.sum(lax.all_gather(value, axis), axis=0)
     return value
 
 

time: 237 us -> 305 us (1.29)
  blocking collectives: 96.5 us -> 139 us
  local copies, waits for them, and re-layouts: 51.3 us -> 70.5 us
  other arithmetic: 17.3 us -> 24.6 us
    all_gather x0 -> x8, blocking collectives: none -> 75.7 us  [one_axis_at_a_time(): value = jnp.sum(lax.all_gather(value, axis), axis=0)]
    psum x8 -> x0, blocking collectives: 60.4 us -> none  [one_axis_at_a_time(): value = lax.psum(value, axis)]
    unnamed x0 -> x4, blocking collectives: none -> 26.7 us
    unnamed x8 -> x42, local copies, waits for them, and re-layouts: 1.54 us -> 20.7 us
    reduce_sum x0 -> x20, other arithmetic: none -> 7.43 us  [one_axis_at_a_time(): value = jnp.sum(lax.all_gather(value, axis), axis=0)]
  transfers between devices with their start and end apart: 1 -> 1, of which waited for: 1 -> 1; matrix products, arithmetic and copies ran while one was open for 6% -> 5% of each run, Pallas kernels for 0% -> 0%
where the time goes in v1:
time: 305 us; the launch traced here: 303 us
  blocking collectives  139 us (46%)
  local copies, waits for them, and re-layouts  70.5 us (23%)
  matrix products  26.1 us (9%)
  other arithmetic  24.6 us (8%)
  waiting for transfers between devices  23.5 us (8%)
  between operations  19.9 us (7%)
    all_gather x8, blocking collectives, one_axis_at_a_time(): value = jnp.sum(lax.all_gather(value, axis), axis=0)  75.7 us
    gather x1, local copies, waits for them, and re-layouts, per_device(): jnp.take_along_axis(capped, jnp.clip(local, 0, vocab_dev - 1)[:, None], a...  45.1 us
    all_gather x4, blocking collectives, gather_in_order(): pieces = lax.all_gather(pieces, axes[k], axis=0, tiled=True)  36.2 us
    unnamed x4, blocking collectives  26.7 us
    dot_general x1, matrix products, per_device(): lax.dot_general(rows, embed, (((1,), (1,)), ((), ())), preferred_element_...  26.1 us
    all_gather x1, waiting for transfers between devices, per_device(): rows = normalize(lax.all_gather(flat, DP_TENSOR, axis=0, tiled=True), gain)  23.5 us
    unnamed x42, local copies, waits for them, and re-layouts  20.7 us
    reduce_sum x20, other arithmetic, one_axis_at_a_time(): value = jnp.sum(lax.all_gather(value, axis), axis=0)  7.43 us
  transfers between devices with their start and end apart: 1, of which 1 were waited for; matrix products, arithmetic and copies ran while one was open for 5% of the time, Pallas kernels for 0%

profile of v1, /device:TPU:0, one launch (start us, length us, event | category | flops | bytes accessed | tf_op | source)
XLA Modules:
  0.0 303.4 jit_solution(15006843411572801947)
XLA Ops:
  7.2 1.5 reshape.313
  8.8 0.8 reshape.428
  9.5 9.8 %all-gather.7 = s32[4,1,8]{2,1,0:T(1,128)S(1)} all-gather(s32[1,1,8]{2,1,0:T(1,128)S(1)} %reshape.428), channel_id=1, replica_groups=mesh['dp_0'=4,'dp_1'=2,'tensor_0'=4,'tensor_1'=4] {'dp_0'}, dimensions={0}, use_global_device_ids=true | all-gather | bytes 160 | tf_op jit(solution)/shard_map/all_gather | solution.py:22
  19.4 11.3 %all-gather.8 = s32[4,4,8]{2,1,0:T(4,128)S(1)} all-gather(s32[1,4,8]{2,1,0:T(4,128)S(1)} %bitcast.56), channel_id=1, replica_groups=mesh['dp_0'=4,'dp_1'=2,'tensor_0'=4,'tensor_1'=4] {'tensor_0'}, dimensions={0}, use_global_device_ids=true | all-gather | bytes 640 | tf_op jit(solution)/shard_map/all_gather | solution.py:22
  30.7 0.1 copy.28
  30.8 13.2 %all-gather.9 = s32[4,16,8]{1,2,0:T(8,128)S(1)} all-gather(s32[1,16,8]{1,2,0:T(8,128)S(1)} %copy.28), channel_id=1, replica_groups=mesh['dp_0'=4,'dp_1'=2,'tensor_0'=4,'tensor_1'=4] {'tensor_1'}, dimensions={0}, use_global_device_ids=true | all-gather | bytes 2560 | tf_op jit(solution)/shard_map/all_gather | solution.py:22
  44.0 0.1 reshape.434
  44.1 1.8 all-gather.10
  45.9 0.1 copy.32
  46.0 0.1 min.24
  46.1 0.1 min.22
  46.3 0.1 copy.30
  46.4 0.1 and.160
  46.5 1.3 dynamic-slice
  47.8 0.1 compare_reduce_fusion.1
  48.3 1.9 fusion.39
  50.2 4.5 %compare_select_fusion.3 = s32[1024,1]{0,1:T(1,128)S(1)} fusion(s32[]{:T(128)} %bitcast.9, s32[]{:T(128)} %bitcast.10, s32[]{:T(128)} %bitcast.11, s32[]{:T(128)} %bitcast.12, s32[]{:T(128)} %bitcast.13, s32[]{:T(128)} %bitcast.15, s32[]{:T(128)} %bitcast.14), kind=kLoop, calls=%fused_computation.23 | loop fusion | flops 60416 | bytes 4124 | tf_op jit(solution)/shard_map/jit(_take)/gather | solution.py:58
  54.8 5.7 %fusion.36 = f32[1024]{0:T(1024)S(1)} fusion(pred[1024]{0:T(1024)(128)(4,1)S(1)} %compare_reduce_fusion, pred[1024]{0:T(1024)(128)(4,1)S(1)} %compare_reduce_fusion.1, pred[1024]{0:T(1024)(128)(4,1)S(1)} %compare_reduce_fusion.2, pred[1024]{0:T(1024)(128)(4,1)S(1)} %compare_reduce_fusion.3, pred[1024]{0:T(1024)(128)(4,1)S(1)} %compare_reduce_fusion.4, ...), kind=kLoop, calls=%fused_computation.92 | loop fusion | flops 73728 | bytes 17444 | tf_op jit(solution)/shard_map/convert_element_type | solution.py:58
  60.5 23.5 %all-gather.14.cloned.1.call-done = bf16[1024,4608]{1,0:T(8,128)(2,1)} async-done(((bf16[8,4608]{1,0:T(8,128)(2,1)}), bf16[1024,4608]{1,0:T(8,128)(2,1)}) %all-gather.14.cloned.1.call-update) | async-done | bytes 9437200 | tf_op jit(solution)/shard_map/all_gather | solution.py:60
  84.0 5.7 %fusion = f32[1024]{0:T(1024)S(1)} fusion(bf16[1024,4608]{1,0:T(8,128)(2,1)} %all-gather.14.cloned.1.call-done), kind=kLoop, calls=%fused_computation.3 | loop fusion | flops 14154752 | bytes 9441280 | tf_op jit(solution)/shard_map/reduce_sum | solution.py:41
  89.7 0.6 copy-done
  90.4 26.1 %exponential_reduce_fusion = (f32[1024]{0:T(1024)S(1)}, f32[1024,2000]{0,1:T(8,128)}) fusion(bf16[2000,4608]{1,0:T(8,128)(2,1)} %param.9, bf16[1024,4608]{1,0:T(8,128)(2,1)S(1)} %copy-done, f32[4608]{0:T(1024)S(1)} %copy-done.1, f32[1024]{0:T(1024)S(1)} %add_rsqrt_fusion), kind=kOutput, calls=%fused_computation.9 | convolution fusion | flops 18899386368 | bytes 36087808 | tf_op jit(solution)/shard_map/dot_general | solution.py:61
  116.5 12.0 %all-gather.3 = f32[4096]{0:T(1024)S(1)} all-gather(f32[1024]{0:T(1024)S(1)} %get-tuple-element.37), channel_id=5, replica_groups=mesh['dp_0'=4,'dp_1'=2,'tensor_0'=4,'tensor_1'=4] {'dp_0'}, dimensions={0}, use_global_device_ids=true | all-gather | bytes 20480 | tf_op jit(solution)/shard_map/all_gather | solution.py:35
  128.5 1.8 all-gather.4
  130.4 12.0 %all-gather.5 = f32[4096]{0:T(1024)S(1)} all-gather(f32[1024]{0:T(1024)S(1)} %reduce_sum.232), channel_id=7, replica_groups=mesh['dp_0'=4,'dp_1'=2,'tensor_0'=4,'tensor_1'=4] {'tensor_0'}, dimensions={0}, use_global_device_ids=true | all-gather | bytes 20480 | tf_op jit(solution)/shard_map/all_gather | solution.py:35
  142.4 12.0 %all-gather.6 = f32[4096]{0:T(1024)S(1)} all-gather(f32[1024]{0:T(1024)S(1)} %reduce_sum.233), channel_id=8, replica_groups=mesh['dp_0'=4,'dp_1'=2,'tensor_0'=4,'tensor_1'=4] {'tensor_1'}, dimensions={0}, use_global_device_ids=true | all-gather | bytes 20480 | tf_op jit(solution)/shard_map/all_gather | solution.py:35
  154.5 45.1 %gather_fusion = f32[1024]{0:T(1024)S(1)} fusion(f32[1024,2000]{0,1:T(8,128)} %get-tuple-element.38, s32[1024]{0:T(1024)S(1)} %bitcast.50), kind=kCustom, calls=%fused_computation | custom fusion | bytes 16384 | tf_op jit(solution)/shard_map/jit(take_along_axis)/gather | solution.py:69
  199.6 12.0 %all-gather.11 = f32[4,1,1024]{2,1,0:T(1,128)S(1)} all-gather(f32[1,1,1024]{2,1,0:T(1,128)S(1)} %fusion.35), channel_id=1, replica_groups=mesh['dp_0'=4,'dp_1'=2,'tensor_0'=4,'tensor_1'=4] {'dp_0'}, dimensions={0}, use_global_device_ids=true | all-gather | bytes 20480 | tf_op jit(solution)/shard_map/all_gather | solution.py:35
  211.6 1.8 all-gather
  213.5 12.0 %all-gather.1 = f32[4096]{0:T(1024)S(1)} all-gather(f32[1024]{0:T(1024)S(1)} %reduce_sum.227), channel_id=3, replica_groups=mesh['dp_0'=4,'dp_1'=2,'tensor_0'=4,'tensor_1'=4] {'tensor_0'}, dimensions={0}, use_global_device_ids=true | all-gather | bytes 20480 | tf_op jit(solution)/shard_map/all_gather | solution.py:35
  225.5 12.0 %all-gather.2 = f32[4096]{0:T(1024)S(1)} all-gather(f32[1024]{0:T(1024)S(1)} %reduce_sum.228), channel_id=4, replica_groups=mesh['dp_0'=4,'dp_1'=2,'tensor_0'=4,'tensor_1'=4] {'tensor_1'}, dimensions={0}, use_global_device_ids=true | all-gather | bytes 20480 | tf_op jit(solution)/shard_map/all_gather | solution.py:35
  237.6 0.7 fusion.37
  239.0 0.7 dynamic-update-slice
  239.7 1.4 dynamic-update-slice.4
  241.1 1.4 dynamic-update-slice.8
  242.5 0.6 dynamic-slice.1
  243.0 7.7 %all-reduce.14 = (f32[4]{0:T(128)S(1)}, f32[4]{0:T(128)S(1)}, f32[4]{0:T(128)S(1)}) all-reduce(f32[4]{0:T(128)S(1)} %dynamic-update-slice, f32[4]{0:T(128)S(1)} %dynamic-update-slice.4, f32[4]{0:T(128)S(1)} %dynamic-update-slice.8), channel_id=1, replica_groups=mesh['dp_0'=4,'dp_1'=2,'tensor_0'=4,'tensor_1'=4] {'dp_0'}, use_global_device_ids=true, to_apply=%add | all-reduce | flops 12 | bytes 96
  250.8 0.6 reduce_sum.236
  251.4 0.6 reduce_sum.241
  252.0 1.4 dynamic-update-slice.1
  253.4 1.4 dynamic-update-slice.5
  254.8 0.6 reduce_sum.246
  255.4 1.4 dynamic-update-slice.9
  256.8 0.6 dynamic-slice.2
  257.4 2.4 all-reduce.15
  259.8 0.6 reduce_sum.237
  260.4 0.6 reduce_sum.242
  261.0 1.4 dynamic-update-slice.2
  262.4 1.4 dynamic-update-slice.6
  263.8 0.6 reduce_sum.247
  264.4 1.4 dynamic-update-slice.10
  265.8 0.6 dynamic-slice.3
  266.4 7.7 %all-reduce.13 = (f32[4]{0:T(128)S(1)}, f32[4]{0:T(128)S(1)}, f32[4]{0:T(128)S(1)}) all-reduce(f32[4]{0:T(128)S(1)} %dynamic-update-slice.2, f32[4]{0:T(128)S(1)} %dynamic-update-slice.6, f32[4]{0:T(128)S(1)} %dynamic-update-slice.10), channel_id=1, replica_groups=mesh['dp_0'=4,'dp_1'=2,'tensor_0'=4,'tensor_1'=4] {'tensor_0'}, use_global_device_ids=true, to_apply=%add.2 | all-reduce | flops 12 | bytes 96
  274.1 0.6 reduce_sum.238
  274.7 0.6 reduce_sum.243
  275.3 1.4 dynamic-update-slice.3
  276.7 1.4 dynamic-update-slice.7
  278.1 0.6 reduce_sum.248
  278.7 1.4 dynamic-update-slice.11
  280.1 0.6 reshape.314
  280.8 8.9 %all-reduce.12 = (f32[4]{0:T(128)S(1)}, f32[4]{0:T(128)S(1)}, f32[4]{0:T(128)S(1)}) all-reduce(f32[4]{0:T(128)S(1)} %dynamic-update-slice.3, f32[4]{0:T(128)S(1)} %dynamic-update-slice.7, f32[4]{0:T(128)S(1)} %dynamic-update-slice.11), channel_id=1, replica_groups=mesh['dp_0'=4,'dp_1'=2,'tensor_0'=4,'tensor_1'=4] {'tensor_1'}, use_global_device_ids=true, to_apply=%add.3 | all-reduce | flops 12 | bytes 96
  289.6 0.6 reduce_sum.239
  290.2 0.7 reduce_sum.244
  292.3 0.6 reduce_sum.249
  (57 shorter events, 0.9 us)
Async XLA Ops:
  7.2 82.6 %copy-start.1 = (f32[4608]{0:T(1024)S(1)}, f32[4608]{0:T(1024)}, u32[]{:S(2)}) copy-start(f32[4608]{0:T(1024)} %param.6) | copy-start | bytes 55300
  7.2 76.8 %all-gather.14.cloned.1.call-start = ((), (), s32[]{:S(2)}) async-start(), calls=%async_computation | async-start | bytes 9510912 | tf_op jit(solution)/shard_map/all_gather | solution.py:60
  84.0 6.4 %copy-start = (bf16[1024,4608]{1,0:T(8,128)(2,1)S(1)}, bf16[1024,4608]{1,0:T(8,128)(2,1)}, u32[]{:S(2)}) copy-start(bf16[1024,4608]{1,0:T(8,128)(2,1)} %all-gather.14.cloned.1.call-done) | copy-start | bytes 28311556
  90.3 152.1 %copy-start.4 = (u32[128]{0:T(128)S(1)}, u32[128]{0:T(128)}, u32[]{:S(2)}) copy-start(u32[128]{0:T(128)} %constant.184) | copy-start | bytes 1540
  90.3 166.4 %copy-start.3 = (u32[128]{0:T(128)S(1)}, u32[128]{0:T(128)}, u32[]{:S(2)}) copy-start(u32[128]{0:T(128)} %constant.189) | copy-start | bytes 1540
  90.4 175.5 %copy-start.2 = (u32[128]{0:T(128)S(1)}, u32[128]{0:T(128)}, u32[]{:S(2)}) copy-start(u32[128]{0:T(128)} %constant.194) | copy-start | bytes 1540
Sparse Core Ops, SparseCore 0:
  11.1 72.8 all-gather.13
